TPU v7x, 256 devices: a whole 4x4x8 slice. The times are simulated.
256 devices in a mesh: trial: 4 (over y), rows: 16 (over z, core), cols: 4 (over x).
Axes of the slice: x: 4, y: 4, z: 8, core: 2. Of those that a mesh axis runs over, the one named last changes fastest.
Arguments:
- weight_gate: float32 [8192, 8192], P(('trial', 'rows'), 'cols'), parts along dimension 0, may hold values from -0.1875 to 0.1875
- moment_gate: float32 [8192, 8192], P(('trial', 'rows'), 'cols'), parts along dimension 0, may hold values from -6 to 6
- square_gate: float32 [8192, 8192], P(('trial', 'rows'), 'cols'), parts along dimension 0, may hold values from 0.1 to 10
- weight_up: float32 [8192, 8192], P(('trial', 'rows'), 'cols'), parts along dimension 0, may hold values from -0.1875 to 0.1875
- moment_up: float32 [8192, 8192], P(('trial', 'rows'), 'cols'), parts along dimension 0, may hold values from -6 to 6
- square_up: float32 [8192, 8192], P(('trial', 'rows'), 'cols'), parts along dimension 0, may hold values from 0.1 to 10
- norm_gain: float32 [8192], P(('trial', 'rows')), parts along dimension 0, may hold values from 0.25 to 1.75
Outputs:
- serving_gate: bfloat16 [8192, 8192], P('trial', 'cols'), parts along dimension 0
- serving_up: bfloat16 [8192, 8192], P('trial', 'cols'), parts along dimension 0
- column_gate: float32 [32768], P(('trial', 'cols')), parts along dimension 0
- column_up: float32 [32768], P(('trial', 'cols')), parts along dimension 0
There are 4 independent parts, one for each index of `trial`. A program takes and returns all parts, laid end to end along the dimension named above; each array names one. Nothing has to cross between parts.
All inputs are finite; a program needn't handle non-finite values. Where the computation divides by a largest or mean magnitude, that divisor is 1e-20 or more.
Results may differ from a plain program's by a relative error of at most 0.001.
Values may be sent and summed in bfloat16 or wider, within the bound.
A program may use at most 128 MiB of HBM per device.

v0:
```python
import jax
import jax.numpy as jnp
from jax import lax
from jax.sharding import PartitionSpec as P

D_MODEL = 2048


learn_rate = 0.02
decay_rate = 0.05
tiny_value = 1e-08


def sent_to_all(shard, axis):
    copies = jnp.broadcast_to(shard, (lax.axis_size(axis), *shard.shape))
    return lax.all_to_all(copies, axis, split_axis=0, concat_axis=0, tiled=True)


def over_copies(shard, axis):
    everything = sent_to_all(shard, axis)
    return jnp.sum(everything, axis=0)


def packed_total(arrays, axis):
    vector, at, done = (jnp.concatenate([a.reshape(-1) for a in arrays]), 0, [])
    so_far = over_copies(vector, axis)
    for a in arrays:
        done.append(so_far[at : at + a.size].reshape(a.shape))
        at += a.size
    return tuple(done)


def sent_together(arrays, axis, dim, along):
    both = jnp.concatenate(arrays, axis=along)
    whole, at, done = (lax.all_gather(both, axis, axis=dim, tiled=True), 0, [])
    for a in arrays:
        done.append(lax.slice_in_dim(whole, at, at + a.shape[along], axis=along))
        at += a.shape[along]
    return tuple(done)


def shards(weight_gate, moment_gate, square_gate, weight_up, moment_up, square_up, norm_gain):
    whole_gate = weight_gate - learn_rate * (
        moment_gate / (jnp.sqrt(square_gate) + tiny_value) + decay_rate * weight_gate
    )
    whole_up = weight_up - learn_rate * (
        moment_up / (jnp.sqrt(square_up) + tiny_value) + decay_rate * weight_up
    )
    whole_gained_gate = whole_gate * norm_gain[:, None]
    whole_gained_up = whole_up * norm_gain[:, None]
    total_gate, total_up = packed_total(
        (jnp.sum(jnp.abs(whole_gained_gate), axis=0), jnp.sum(jnp.abs(whole_gained_up), axis=0)),
        "rows",
    )
    column_gate = total_gate / D_MODEL
    column_up = total_up / D_MODEL
    narrow_gate, narrow_up = (
        (whole_gained_gate / column_gate).astype(jnp.bfloat16),
        (whole_gained_up / column_up).astype(jnp.bfloat16),
    )
    serving_gate, serving_up = sent_together((narrow_gate, narrow_up), "rows", 0, 1)
    return (serving_gate, serving_up, column_gate, column_up)


def solution(mesh):
    return jax.shard_map(
        shards,
        mesh=mesh,
        in_specs=(
            P(("trial", "rows"), "cols"),
            P(("trial", "rows"), "cols"),
            P(("trial", "rows"), "cols"),
            P(("trial", "rows"), "cols"),
            P(("trial", "rows"), "cols"),
            P(("trial", "rows"), "cols"),
            P(("trial", "rows")),
        ),
        out_specs=(
            P("trial", "cols"),
            P("trial", "cols"),
            P(("trial", "cols")),
            P(("trial", "cols")),
        ),
        check_vma=False,
    )
```

profile of v0, /device:TPU:1, one launch (start us, length us, event | category | flops | bytes accessed | tf_op | source)
XLA Modules:
  0.0 145.8 jit_solution(15943611371446111643)
XLA Ops:
  7.2 0.0 all-gather.2.cloned.1.call-start
  7.2 4.0 %abs_reduce_fusion.1 = (f32[2048]{0:T(1024)S(1)}, f32[128,2048]{1,0:T(8,128)S(1)}, f32[2048]{0:T(1024)S(1)}, f32[128,2048]{1,0:T(8,128)S(1)}) fusion(f32[128]{0:T(128)} %param.13, f32[128,2048]{1,0:T(8,128)} %param.7, f32[128,2048]{1,0:T(8,128)} %param.8, f32[128,2048]{1,0:T(8,128)} %param.9, f32[128,2048]{1,0:T(8,128)} %param.10, f32[128,2048]{1,0:T(8,128)} %param.11, ...), kind=kLoop, calls=%fused_computation.5 | loop fusion | flops 4714496 | bytes 8405504 | tf_op jit(solution)/shard_map/reduce_sum | solution.py:52
  11.3 0.2 broadcast_in_dim.2
  11.5 21.4 %all_to_all.6 = f32[16,1,4096]{2,1,0:T(1,128)S(1)} all-to-all(f32[16,1,4096]{2,1,0:T(1,128)S(1)} %broadcast_in_dim.2), channel_id=1, replica_groups=mesh['trial'=4,'rows'=16,'cols'=4] {'rows'}, dimensions={0} | all-to-all | bytes 524288 | tf_op jit(solution)/shard_map/all_to_all | solution.py:16
  32.8 0.2 reduce_sum.29
  33.0 0.0 copy-start
  33.0 0.0 copy-start.1
  33.0 0.2 divide_convert_fusion
  33.2 1.1 pad_maximum_fusion
  34.3 0.0 all-gather.2.cloned.1.call-update
  34.3 92.7 %all-gather.2.cloned.1.call-done = bf16[2048,4096]{1,0:T(8,128)(2,1)} async-done(((bf16[128,4096]{1,0:T(8,128)(2,1)}), bf16[2048,4096]{1,0:T(8,128)(2,1)}) %all-gather.2.cloned.1.call-update) | async-done | bytes 16777232 | tf_op jit(solution)/shard_map/all_gather | solution.py:35
  127.0 11.9 %fusion = (bf16[2048,2048]{1,0:T(8,128)(2,1)}, bf16[2048,2048]{1,0:T(8,128)(2,1)}) fusion(bf16[2048,4096]{1,0:T(8,128)(2,1)} %all-gather.2.cloned.1.call-done), kind=kLoop, calls=%fused_computation.10 | loop fusion | bytes 33554432 | tf_op jit(solution)/shard_map/slice | solution.py:37
  139.0 0.0 copy-done
  139.0 0.0 copy-done.1
  (2 shorter events, 0.0 us)
Async XLA Ops:
  7.2 119.9 %all-gather.2.cloned.1.call-start = ((), (), s32[]{:S(2)}) async-start(), calls=%async_computation.1 | async-start | bytes 17825792 | tf_op jit(solution)/shard_map/all_gather | solution.py:35
  33.0 106.0 %copy-start = (f32[2048]{0:T(1024)}, f32[2048]{0:T(1024)S(1)}, u32[]{:S(2)}) copy-start(f32[2048]{0:T(1024)S(1)} %get-tuple-element.10) | copy-start | bytes 24580
  33.0 106.0 %copy-start.1 = (f32[2048]{0:T(1024)}, f32[2048]{0:T(1024)S(1)}, u32[]{:S(2)}) copy-start(f32[2048]{0:T(1024)S(1)} %get-tuple-element.11) | copy-start | bytes 24580
Sparse Core Ops, SparseCore 0:
  34.4 92.5 all-gather.1
where the time goes:
time: 146 us
  waiting for transfers between devices  92.7 us (63%)
  blocking collectives  21.4 us (15%)
  between operations  14.1 us (10%)
  local copies, waits for them, and re-layouts  12.2 us (8%)
  other arithmetic  5.47 us (4%)
    all_gather x1, waiting for transfers between devices, sent_together(): whole, at, done = (lax.all_gather(both, axis, axis=dim, tiled=True), 0, [])  92.7 us
    all_to_all x1, blocking collectives, sent_to_all(): return lax.all_to_all(copies, axis, split_axis=0, concat_axis=0, tiled=True)  21.4 us
    slice x1, local copies, waits for them, and re-layouts, sent_together(): done.append(lax.slice_in_dim(whole, at, at + a.shape[along], axis=along))  11.9 us
    reduce_sum x1, other arithmetic, shards(): jnp.sum(jnp.abs(whole_gained_gate), axis=0)  4.03 us
  transfers between devices with their start and end apart: 1, of which 1 were waited for; matrix products, arithmetic and copies ran while one was open for 0% of the time, Pallas kernels for 0%

commit v1 on v0

v1 whole, which is shorter than its diff:
```python
import functools

import jax
import jax.numpy as jnp
from jax import lax
from jax.experimental import pallas as pl
from jax.experimental.pallas import tpu as pltpu
from jax.sharding import PartitionSpec as P

D_MODEL = 2048
learn_rate = 0.02
decay_rate = 0.05
tiny_value = 1e-08

MESH = pl.DeviceIdType.MESH
F32, BF16 = jnp.float32, jnp.bfloat16

CHIPS = 8
PIECES = 4
CHUNK = 512


def gather_kernel(
    wg, mg, sg, wu, mu, su, gain_hbm,
    out_g, out_u, scale_g, scale_u,
    held, plain, gain, gain_t, part, pair_in, slots,
    load_sem, gain_sem, pair_s, pair_r, slot_s, slot_r, scale_s, scale_r,
    right_s, right_r, left_s, left_r, side_s, side_r,
):
    rows, width = wg.shape
    half = width // 2
    me = lax.axis_index("rows")
    chip, core = me // 2, me % 2
    partner = chip * 2 + (1 - core)
    outs, scales = (out_g, out_u), (scale_g, scale_u)
    sources = ((wg, mg, sg), (wu, mu, su))

    def at(c):
        return lax.rem(c + CHIPS, CHIPS)

    def peer(distance):
        return at(chip + distance) * 2 + core

    gain_copy = pltpu.make_async_copy(gain_hbm, gain, gain_sem)
    gain_copy.start()
    loads = []
    for q in range(2):
        for k in range(width // CHUNK):
            cols = pl.ds(k * CHUNK, CHUNK)
            trio = [
                pltpu.make_async_copy(
                    sources[q][i].at[:, cols], held.at[q, i, :, cols], load_sem.at[q, k, i]
                )
                for i in range(3)
            ]
            for copy in trio:
                copy.start()
            loads.append(trio)

    barrier = pltpu.get_barrier_semaphore()
    pl.semaphore_signal(barrier, inc=1, device_id={"rows": partner}, device_id_type=MESH)
    for d in range(1, CHIPS):
        pl.semaphore_signal(barrier, inc=1, device_id={"rows": peer(d)}, device_id_type=MESH)

    gain_copy.wait()
    gain_t[...] = jnp.broadcast_to(gain[...], (rows, rows)).T

    def update(q, k):
        for copy in loads[q * (width // CHUNK) + k]:
            copy.wait()

        @pl.loop(k * CHUNK // 128, (k + 1) * CHUNK // 128)
        def _(j):
            cols = pl.ds(pl.multiple_of(j * 128, 128), 128)
            w = held[q, 0, :, cols]
            m = held[q, 1, :, cols]
            s = held[q, 2, :, cols]
            whole = w - learn_rate * (m / (jnp.sqrt(s) + tiny_value) + decay_rate * w)
            gained = whole * gain_t[...]
            plain[q, :, cols] = gained
            part[q, :, cols] = jnp.sum(jnp.abs(gained), axis=0, keepdims=True)

    def cols_of(h):
        which = (core + h) % 2
        return pl.ds(pl.multiple_of(which * half, half), half)

    mine, other = cols_of(0), cols_of(1)

    def pair_copy(q):
        return pltpu.make_async_remote_copy(
            src_ref=part.at[q, :, other], dst_ref=pair_in.at[q],
            send_sem=pair_s.at[q], recv_sem=pair_r.at[q],
            device_id={"rows": partner}, device_id_type=MESH,
        )

    def slot_copy(q, d):
        return pltpu.make_async_remote_copy(
            src_ref=slots.at[q, 0], dst_ref=slots.at[q, d],
            send_sem=slot_s.at[q, d - 1], recv_sem=slot_r.at[q, d - 1],
            device_id={"rows": peer(d)}, device_id_type=MESH,
        )

    def scale_copy(q, where):
        return pltpu.make_async_remote_copy(
            src_ref=scales[q].at[:, where], dst_ref=scales[q].at[:, where],
            send_sem=scale_s.at[q], recv_sem=scale_r.at[q],
            device_id={"rows": partner}, device_id_type=MESH,
        )

    def block(q, origin_chip, origin_core, h):
        start = pl.multiple_of((origin_chip * 2 + origin_core) * rows, rows)
        return outs[q].at[pl.ds(start, rows), cols_of(h)]

    def ring_copy(step, p, sign):
        q, h = p // 2, p % 2
        ref = block(q, at(chip - sign * step), core, h)
        s, r = (right_s, right_r) if sign > 0 else (left_s, left_r)
        return pltpu.make_async_remote_copy(
            src_ref=ref, dst_ref=ref,
            send_sem=s.at[step, p], recv_sem=r.at[step, p],
            device_id={"rows": peer(sign)}, device_id_type=MESH,
        )

    def ring_arrival(step, p, sign):
        q, h = p // 2, p % 2
        ref = block(q, at(chip - sign * (step + 1)), core, h)
        s, r = (right_s, right_r) if sign > 0 else (left_s, left_r)
        return pltpu.make_async_remote_copy(
            src_ref=ref, dst_ref=ref,
            send_sem=s.at[step, p], recv_sem=r.at[step, p],
            device_id={"rows": peer(sign)}, device_id_type=MESH,
        )

    def side_copy(offset, p, arriving=False):
        q, h = p // 2, p % 2
        if arriving:
            ref = block(q, at(chip + offset), 1 - core, 1 - h)
            ref = outs[q].at[
                pl.ds(pl.multiple_of((at(chip + offset) * 2 + 1 - core) * rows, rows), rows),
                cols_of(1 - h),
            ]
        else:
            ref = block(q, at(chip + offset), core, h)
        index = offset % CHIPS
        return pltpu.make_async_remote_copy(
            src_ref=ref, dst_ref=ref,
            send_sem=side_s.at[index, p], recv_sem=side_r.at[index, p],
            device_id={"rows": partner}, device_id_type=MESH,
        )

    def pair_sum(q):
        pair_copy(q).wait_recv()
        slots[q, 0] = part[q, :, mine] + pair_in[q]
        for d in (4, 3, 5, 2, 6, 1, 7):
            slot_copy(q, d).start()

    def total(q):
        for d in range(1, CHIPS):
            slot_copy(q, d).wait_recv()
        acc = jnp.zeros((1, half), F32)
        for c in range(CHIPS):
            acc = acc + slots[q, at(chip - c)]
        scales[q][:, mine] = acc / D_MODEL
        scale_copy(q, mine).start()

    def narrow(p):
        q, h = p // 2, p % 2
        which = (core + h) % 2
        start = pl.multiple_of(me * rows, rows)

        @pl.loop(0, half // 128)
        def _(j):
            cols = pl.ds(pl.multiple_of(which * half + j * 128, 128), 128)
            inverse = 1.0 / scales[q][:, cols]
            outs[q][pl.ds(start, rows), cols] = (plain[q, :, cols] * inverse).astype(BF16)

    def send_own(p):
        narrow(p)
        ring_copy(0, p, 1).start()
        ring_copy(0, p, -1).start()
        side_copy(0, p).start()

    for k in range(width // CHUNK):
        update(0, k)
    pl.semaphore_wait(barrier, CHIPS)
    pair_copy(0).start()
    update(1, 0)
    pair_sum(0)
    for k in range(1, width // CHUNK):
        update(1, k)
    pair_copy(1).start()
    pair_sum(1)
    total(0)
    send_own(0)
    scale_copy(0, other).wait_recv()
    send_own(1)
    total(1)
    send_own(2)
    scale_copy(1, other).wait_recv()
    send_own(3)

    sent = [(0, p, sign) for p in range(PIECES) for sign in (1, -1)]
    handed = [(0, p) for p in range(PIECES)]
    for step in range(CHIPS // 2):
        for p in range(PIECES):
            for sign in (1, -1):
                last = step == CHIPS // 2 - 1
                if last and (p < PIECES // 2) != (sign > 0):
                    continue
                ring_arrival(step, p, sign).wait_recv()
                on = step + 1
                if on < CHIPS // 2 - 1 or (on == CHIPS // 2 - 1 and (p < PIECES // 2) == (sign > 0)):
                    ring_copy(on, p, sign).start()
                    sent.append((on, p, sign))
                offset = -sign * (step + 1)
                side_copy(offset, p).start()
                handed.append((offset, p))
    for offset, p in handed:
        side_copy(offset, p, arriving=True).wait_recv()
    for step, p, sign in sent:
        ring_copy(step, p, sign).wait_send()
    for offset, p in handed:
        side_copy(offset, p).wait_send()
    for q in range(2):
        pair_copy(q).wait_send()
        scale_copy(q, mine).wait_send()
        for d in range(1, CHIPS):
            slot_copy(q, d).wait_send()


def write_kernel(g, u, a, b, g_out, u_out, a_out, b_out, sems):
    parts = 4
    rows = g.shape[0] // parts
    copies = [
        pltpu.make_async_copy(a, a_out, sems.at[2 * parts]),
        pltpu.make_async_copy(b, b_out, sems.at[2 * parts + 1]),
    ]
    for i, (src, dst) in enumerate(((g, g_out), (u, u_out))):
        for k in range(parts):
            where = pl.ds(k * rows, rows)
            copies.append(pltpu.make_async_copy(src.at[where], dst.at[where], sems.at[i * parts + k]))
    for copy in copies:
        copy.start()
    for copy in copies:
        copy.wait()


def shards(weight_gate, moment_gate, square_gate, weight_up, moment_up, square_up, norm_gain):
    rows, width = weight_gate.shape
    total_rows = rows * lax.axis_size("rows")
    half = width // 2
    any_spec = pl.BlockSpec(memory_space=pl.ANY)
    hbm_spec = pl.BlockSpec(memory_space=pltpu.HBM)
    vmem_spec = pl.BlockSpec(memory_space=pltpu.VMEM)
    dma = pltpu.SemaphoreType.DMA
    g, u, a, b = pl.pallas_call(
        gather_kernel,
        name="gather",
        out_shape=(
            pltpu.VMEM((total_rows, width), BF16),
            pltpu.VMEM((total_rows, width), BF16),
            pltpu.VMEM((1, width), F32),
            pltpu.VMEM((1, width), F32),
        ),
        in_specs=[hbm_spec] * 7,
        out_specs=(vmem_spec,) * 4,
        scratch_shapes=[
            pltpu.VMEM((2, 3, rows, width), F32),
            pltpu.VMEM((2, rows, width), F32),
            pltpu.VMEM((1, rows), F32),
            pltpu.VMEM((rows, rows), F32),
            pltpu.VMEM((2, 1, width), F32),
            pltpu.VMEM((2, 1, half), F32),
            pltpu.VMEM((2, CHIPS, 1, half), F32),
            dma((2, width // CHUNK, 3)), dma,
            dma((2,)), dma((2,)),
            dma((2, CHIPS - 1)), dma((2, CHIPS - 1)),
            dma((2,)), dma((2,)),
            dma((CHIPS // 2, PIECES)), dma((CHIPS // 2, PIECES)),
            dma((CHIPS // 2, PIECES)), dma((CHIPS // 2, PIECES)),
            dma((CHIPS, PIECES)), dma((CHIPS, PIECES)),
        ],
        compiler_params=pltpu.CompilerParams(
            collective_id=0, has_side_effects=True, vmem_limit_bytes=14 * 2**20
        ),
    )(weight_gate, moment_gate, square_gate, weight_up, moment_up, square_up, norm_gain.reshape(1, rows))
    g, u, a, b = pl.pallas_call(
        write_kernel,
        name="write",
        out_shape=(
            jax.ShapeDtypeStruct((total_rows, width), BF16),
            jax.ShapeDtypeStruct((total_rows, width), BF16),
            jax.ShapeDtypeStruct((1, width), F32),
            jax.ShapeDtypeStruct((1, width), F32),
        ),
        in_specs=[vmem_spec] * 4,
        out_specs=(any_spec,) * 4,
        scratch_shapes=[dma((10,))],
        compiler_params=pltpu.CompilerParams(vmem_limit_bytes=2 * 2**20),
    )(g, u, a, b)
    return g, u, a.reshape(width), b.reshape(width)


def solution(mesh):
    return jax.shard_map(
        shards,
        mesh=mesh,
        in_specs=(
            P(("trial", "rows"), "cols"),
            P(("trial", "rows"), "cols"),
            P(("trial", "rows"), "cols"),
            P(("trial", "rows"), "cols"),
            P(("trial", "rows"), "cols"),
            P(("trial", "rows"), "cols"),
            P(("trial", "rows")),
        ),
        out_specs=(
            P("trial", "cols"),
            P("trial", "cols"),
            P(("trial", "cols")),
            P(("trial", "cols")),
        ),
        check_vma=False,
    )
```

time: 146 us -> 114 us (0.78)
  Pallas kernels: 0 us -> 105 us
  waiting for transfers between devices: 92.7 us -> 0 us
  blocking collectives: 21.4 us -> 0 us
  between operations: 14.1 us -> 0.66 us
  other arithmetic: 5.47 us -> 0 us
  local copies, waits for them, and re-layouts: 12.2 us -> 7.99 us
    pallas_call x0 -> x2, Pallas kernels: none -> 105 us  [the longest x1 99.2 us: shards(): pl.pallas_call(gather_kernel, name='gather', out_shape=(pltpu.VMEM((total...]
    all_gather x1 -> x0, waiting for transfers between devices: 92.7 us -> none  [sent_together(): whole, at, done = (lax.all_gather(both, axis, axis=dim, tiled=True), 0, [])]
    all_to_all x1 -> x0, blocking collectives: 21.4 us -> none  [sent_to_all(): return lax.all_to_all(copies, axis, split_axis=0, concat_axis=0, tiled=True)]
    slice x1 -> x0, local copies, waits for them, and re-layouts: 11.9 us -> none  [sent_together(): done.append(lax.slice_in_dim(whole, at, at + a.shape[along], axis=along))]
    unnamed x4 -> x14, local copies, waits for them, and re-layouts: 0.01 us -> 7.99 us
    reduce_sum x2 -> x0, other arithmetic: 4.21 us -> none  [the longest x1 4.03 us: shards(): jnp.sum(jnp.abs(whole_gained_gate), axis=0)]
  transfers between devices with their start and end apart: 1 -> 0, of which waited for: 1 -> 0; matrix products, arithmetic and copies ran while one was open for 0% -> 0% of each run, Pallas kernels for 0% -> 0%
where the time goes in v1:
time: 114 us
  Pallas kernels  105 us (92%)
  local copies, waits for them, and re-layouts  7.99 us (7%)
    pallas_call x1, Pallas kernels, shards(): pl.pallas_call(gather_kernel, name='gather', out_shape=(pltpu.VMEM((total...  99.2 us
    unnamed x14, local copies, waits for them, and re-layouts  7.99 us
    pallas_call x1, Pallas kernels, shards(): pl.pallas_call(write_kernel, name='write', out_shape=(jax.ShapeDtypeStruc...  5.95 us

profile of v1, /device:TPU:1, one launch (start us, length us, event | category | flops | bytes accessed | tf_op | source)
XLA Modules:
  0.0 113.8 jit_solution(15908614410304195087)
XLA Ops:
  0.6 0.0 copy-start
  0.6 1.2 %copy-done = f32[128,2048]{1,0:T(8,128)S(1)} copy-done((f32[128,2048]{1,0:T(8,128)S(1)}, f32[128,2048]{1,0:T(8,128)}, u32[]{:S(2)}) %copy-start) | copy-done | bytes 1048600
  1.9 0.0 copy-start.1
  1.9 1.2 %copy-done.1 = f32[128,2048]{1,0:T(8,128)S(1)} copy-done((f32[128,2048]{1,0:T(8,128)S(1)}, f32[128,2048]{1,0:T(8,128)}, u32[]{:S(2)}) %copy-start.1) | copy-done | bytes 1048600
  3.1 0.0 copy-start.2
  3.1 1.2 %copy-done.2 = f32[128,2048]{1,0:T(8,128)S(1)} copy-done((f32[128,2048]{1,0:T(8,128)S(1)}, f32[128,2048]{1,0:T(8,128)}, u32[]{:S(2)}) %copy-start.2) | copy-done | bytes 1048600
  4.3 0.0 copy-start.3
  4.3 1.2 %copy-done.3 = f32[128,2048]{1,0:T(8,128)S(1)} copy-done((f32[128,2048]{1,0:T(8,128)S(1)}, f32[128,2048]{1,0:T(8,128)}, u32[]{:S(2)}) %copy-start.3) | copy-done | bytes 1048600
  5.5 0.0 copy-start.4
  5.5 1.2 %copy-done.4 = f32[128,2048]{1,0:T(8,128)S(1)} copy-done((f32[128,2048]{1,0:T(8,128)S(1)}, f32[128,2048]{1,0:T(8,128)}, u32[]{:S(2)}) %copy-start.4) | copy-done | bytes 1048600
  6.8 0.0 copy-start.5
  6.8 1.2 %copy-done.5 = f32[128,2048]{1,0:T(8,128)S(1)} copy-done((f32[128,2048]{1,0:T(8,128)S(1)}, f32[128,2048]{1,0:T(8,128)}, u32[]{:S(2)}) %copy-start.5) | copy-done | bytes 1048600
  8.0 0.0 copy-start.6
  8.0 0.7 copy-done.6
  8.6 99.2 %gather.1 = (bf16[2048,2048]{1,0:T(8,128)(2,1)S(1)}, bf16[2048,2048]{1,0:T(8,128)(2,1)S(1)}, f32[1,2048]{1,0:T(1,128)S(1)}, f32[1,2048]{1,0:T(1,128)S(1)}) custom-call(f32[128,2048]{1,0:T(8,128)S(1)} %copy-done, f32[128,2048]{1,0:T(8,128)S(1)} %copy-done.1, f32[128,2048]{1,0:T(8,128)S(1)} %copy-done.2, f32[128,2048]{1,0:T(8,128)S(1)} %copy-done.3, ...), custom_call_target="tpu_custom_call" | custom-call | tf_op jit(solution)/shard_map/gather/pallas_call | solution.py:256
  107.8 6.0 %write.1 = (bf16[2048,2048]{1,0:T(8,128)(2,1)}, bf16[2048,2048]{1,0:T(8,128)(2,1)}, f32[1,2048]{1,0:T(1,128)}, f32[1,2048]{1,0:T(1,128)}) custom-call(bf16[2048,2048]{1,0:T(8,128)(2,1)S(1)} %get-tuple-element.12.g, bf16[2048,2048]{1,0:T(8,128)(2,1)S(1)} %get-tuple-element.13.u, f32[1,2048]{1,0:T(1,128)S(1)} %get-tuple-element.14.a, ...), custom_call_target="tpu_custom_call" | custom-call | tf_op jit(solution)/shard_map/write/pallas_call | solution.py:287
Async XLA Ops:
  0.6 1.2 %copy-start = (f32[128,2048]{1,0:T(8,128)S(1)}, f32[128,2048]{1,0:T(8,128)}, u32[]{:S(2)}) copy-start(f32[128,2048]{1,0:T(8,128)} %wg.1) | copy-start | bytes 3145732
  1.9 1.2 %copy-start.1 = (f32[128,2048]{1,0:T(8,128)S(1)}, f32[128,2048]{1,0:T(8,128)}, u32[]{:S(2)}) copy-start(f32[128,2048]{1,0:T(8,128)} %mg.1) | copy-start | bytes 3145732
  3.1 1.2 %copy-start.2 = (f32[128,2048]{1,0:T(8,128)S(1)}, f32[128,2048]{1,0:T(8,128)}, u32[]{:S(2)}) copy-start(f32[128,2048]{1,0:T(8,128)} %sg.1) | copy-start | bytes 3145732
  4.3 1.2 %copy-start.3 = (f32[128,2048]{1,0:T(8,128)S(1)}, f32[128,2048]{1,0:T(8,128)}, u32[]{:S(2)}) copy-start(f32[128,2048]{1,0:T(8,128)} %wu.1) | copy-start | bytes 3145732
  5.5 1.2 %copy-start.4 = (f32[128,2048]{1,0:T(8,128)S(1)}, f32[128,2048]{1,0:T(8,128)}, u32[]{:S(2)}) copy-start(f32[128,2048]{1,0:T(8,128)} %mu.1) | copy-start | bytes 3145732
  6.8 1.2 %copy-start.5 = (f32[128,2048]{1,0:T(8,128)S(1)}, f32[128,2048]{1,0:T(8,128)}, u32[]{:S(2)}) copy-start(f32[128,2048]{1,0:T(8,128)} %su.1) | copy-start | bytes 3145732
  8.0 0.7 copy-start.6

commit v2 on v0

v2 whole, which is shorter than its diff:
```python
import functools

import jax
import jax.numpy as jnp
from jax import lax
from jax.experimental import pallas as pl
from jax.experimental.pallas import tpu as pltpu
from jax.sharding import PartitionSpec as P

D_MODEL = 2048
learn_rate = 0.02
decay_rate = 0.05
tiny_value = 1e-08

MESH = pl.DeviceIdType.MESH
F32, BF16 = jnp.float32, jnp.bfloat16

CHIPS = 8
GROUPS = 4
PIECES = 8
CHUNK = 512
AHEAD = 3
RAW = 48
SLICE = 16


def gather_kernel(
    wg, mg, sg, wu, mu, su, gain_hbm,
    out_g, out_u, scale_g, scale_u,
    held, plain, gain, gain_t, part, slots, pair_in, pair_slots, raw_in,
    load_sem, gain_sem, pair_s, pair_r, slot_s, slot_r, scale_s, scale_r,
    raw_s, raw_r, rest_s, rest_r, ring_s, ring_r, last_r, side_s, side_r,
):
    rows, width = wg.shape
    wide = width * 2 // GROUPS
    half = wide // 2
    chunks = width // CHUNK
    me = lax.axis_index("rows")
    chip, core = me // 2, me % 2
    partner = chip * 2 + (1 - core)
    outs, scales = (out_g, out_u), (scale_g, scale_u)
    sources = ((wg, mg, sg), (wu, mu, su))

    def at(c):
        return lax.rem(c + CHIPS, CHIPS)

    def device(r):
        return dict(device_id={"rows": r}, device_id_type=MESH)

    def take(ref, sem):
        pltpu.make_async_copy(ref, ref, sem).wait()

    def load(n):
        q, k = n // chunks, n % chunks
        cols = pl.ds(k * CHUNK, CHUNK)
        for i in range(3):
            pltpu.make_async_copy(
                sources[q][i].at[:, cols], held.at[q, i, :, cols], load_sem.at[n % (AHEAD + 1)]
            ).start()

    gain_copy = pltpu.make_async_copy(gain_hbm, gain, gain_sem)
    gain_copy.start()
    for n in range(AHEAD):
        load(n)

    barrier = pltpu.get_barrier_semaphore()
    for d in (4, 3, 5, 2, 6, 1, 7):
        for h in range(2):
            pl.semaphore_signal(barrier, inc=1, **device(at(chip + d) * 2 + h))
    pl.semaphore_signal(barrier, inc=1, **device(partner))

    gain_copy.wait()
    gain_t[...] = jnp.broadcast_to(gain[...], (rows, rows)).T

    def update(n):
        q, k = n // chunks, n % chunks
        if n + AHEAD < 2 * chunks:
            load(n + AHEAD)
        block = held.at[q, :, :, pl.ds(k * CHUNK, CHUNK)]
        pltpu.make_async_copy(block, block, load_sem.at[n % (AHEAD + 1)]).wait()

        @pl.loop(k * CHUNK // 128, (k + 1) * CHUNK // 128)
        def _(j):
            cols = pl.ds(pl.multiple_of(j * 128, 128), 128)
            w = held[q, 0, :, cols]
            m = held[q, 1, :, cols]
            s = held[q, 2, :, cols]
            whole = w - learn_rate * (m / (jnp.sqrt(s) + tiny_value) + decay_rate * w)
            gained = whole * gain_t[...]
            plain[q, :, cols] = gained
            part[q, :, cols] = jnp.sum(jnp.abs(gained), axis=0, keepdims=True)

    def start_of(g, h):
        return (g % (GROUPS // 2)) * wide + (core + h) % 2 * half

    def cols_of(g, h):
        return pl.ds(pl.multiple_of(start_of(g, h), half), half)

    far_first = (4, 3, 5, 2, 6, 1, 7)

    def part_of(g, where):
        return part.at[g // (GROUPS // 2), :, where]

    def first_copy(where, target):
        return pltpu.make_async_remote_copy(
            src_ref=part_of(0, where), dst_ref=slots.at[me],
            send_sem=slot_s, recv_sem=slot_r.at[0], **device(target),
        )

    def send_first():
        for d in far_first:
            for h in range(2):
                first_copy(pl.ds(h * half, half), at(chip + d) * 2 + h).start()
        first_copy(cols_of(0, 1), partner).start()
        slots[me] = part[0, :, cols_of(0, 0)]

    def pair_copy(g):
        return pltpu.make_async_remote_copy(
            src_ref=part_of(g, cols_of(g, 1)), dst_ref=pair_in.at[g - 1],
            send_sem=pair_s, recv_sem=pair_r.at[g - 1], **device(partner),
        )

    def send_pair(g):
        pair_copy(g).wait_recv()
        pair_slots[g - 1, chip] = part[g // (GROUPS // 2), :, cols_of(g, 0)] + pair_in[g - 1]
        ref = pair_slots.at[g - 1, chip]
        for d in far_first:
            pltpu.make_async_remote_copy(
                src_ref=ref, dst_ref=ref, send_sem=slot_s, recv_sem=slot_r.at[g],
                **device(at(chip + d) * 2 + core),
            ).start()

    def scale_copy(g, h):
        ref = scales[g // (GROUPS // 2)].at[:, cols_of(g, h)]
        return pltpu.make_async_remote_copy(
            src_ref=ref, dst_ref=ref, send_sem=scale_s, recv_sem=scale_r.at[g],
            **device(partner),
        )

    def total(g):
        mine = slots if g == 0 else pair_slots.at[g - 1]
        count = mine.shape[0]
        take(mine.at[pl.ds(0, count - 1)], slot_r.at[g])
        acc = mine[0]
        for r in range(1, count):
            acc = acc + mine[r]
        scales[g // (GROUPS // 2)][:, cols_of(g, 0)] = acc / D_MODEL
        scale_copy(g, 0).start()

    def rows_of(offset, first=0, count=rows):
        start = (at(chip + offset) * 2 + core) * rows + first
        return pl.ds(pl.multiple_of(start, SLICE), count)

    def place(offset, q, p=None, first=0, count=rows):
        if p is None:
            return outs[q].at[rows_of(offset, first, count)]
        return outs[q].at[rows_of(offset, first, count), cols_of(p // 2, p % 2)]

    def neighbour(way):
        return device(at(chip + 1 - 2 * way) * 2 + core)

    def onward(ref, way, recv_sem, send_sem=None):
        return pltpu.make_async_remote_copy(
            src_ref=ref, dst_ref=ref, send_sem=ring_s.at[way] if send_sem is None else send_sem,
            recv_sem=recv_sem, **neighbour(way),
        )

    def raw_copy(i, way):
        some = pl.ds(i * SLICE, SLICE)
        return pltpu.make_async_remote_copy(
            src_ref=plain.at[0, some, cols_of(0, 0)], dst_ref=raw_in.at[way, some],
            send_sem=raw_s, recv_sem=raw_r.at[way], **neighbour(way),
        )

    def send_raw(i):
        if i < RAW // SLICE:
            for way in range(2):
                raw_copy(i, way).start()

    def side_copy(ref):
        return pltpu.make_async_remote_copy(
            src_ref=ref, dst_ref=ref, send_sem=side_s, recv_sem=side_r, **device(partner)
        )

    def narrow(p):
        g, h = p // 2, p % 2
        q = g // (GROUPS // 2)
        first = start_of(g, h)
        start = pl.multiple_of(me * rows, rows)

        @pl.loop(0, half // 128)
        def _(j):
            cols = pl.ds(pl.multiple_of(first + j * 128, 128), 128)
            inverse = 1.0 / scales[q][:, cols]
            outs[q][pl.ds(start, rows), cols] = (plain[q, :, cols] * inverse).astype(BF16)

    def send_own(p):
        narrow(p)
        q = p * 2 // PIECES
        for way in range(2):
            if p == 0:
                onward(place(0, q, p, RAW, rows - RAW), way, rest_r.at[way], rest_s).start()
            else:
                onward(place(0, q, p), way, ring_r.at[way, 0, q]).start()
        side_copy(place(0, q, p)).start()

    each = 2 * chunks // GROUPS
    for n in range(each):
        update(n)
    pl.semaphore_wait(barrier, 2 * CHIPS - 1)
    send_first()
    send_raw(0)
    for g in range(1, GROUPS):
        for n in range(g * each, (g + 1) * each):
            update(n)
        pair_copy(g).start()
        if g > 1:
            send_pair(g - 1)
            send_raw(g - 1)
    send_pair(GROUPS - 1)
    total(0)
    send_own(0)
    scale_copy(0, 1).wait_recv()
    send_own(1)
    for g in range(1, GROUPS):
        total(g)
        send_own(2 * g)
        scale_copy(g, 1).wait_recv()
        send_own(2 * g + 1)
    def scale_raw(way):
        take(raw_in.at[way, pl.ds(0, RAW)], raw_r.at[way])
        take(place(0, 0, 0, RAW, rows - RAW), rest_r.at[way])

        @pl.loop(0, half // 128)
        def _(j):
            here = pl.ds(pl.multiple_of(j * 128, 128), 128)
            cols = pl.ds(pl.multiple_of(start_of(0, 0) + j * 128, 128), 128)
            inverse = 1.0 / scale_g[:, cols]
            out_g[rows_of(2 * way - 1, 0, RAW), cols] = (
                raw_in[way, pl.ds(0, RAW), here] * inverse
            ).astype(BF16)

    steps = CHIPS // 2
    for step in range(steps - 1):
        for q in range(2):
            for way in range(2):
                offset = (2 * way - 1) * (step + 1)
                whole = place(offset, q)
                if step == 0 and q == 0:
                    scale_raw(way)
                    take(outs[q].at[rows_of(offset), pl.ds(0, width - half)], ring_r.at[way, step, q])
                else:
                    take(whole, ring_r.at[way, step, q])
                if step + 1 < steps - 1:
                    onward(whole, way, ring_r.at[way, step + 1, q]).start()
                elif q == way:
                    for i in range(PIECES // 2):
                        onward(place(offset, q, q * PIECES // 2 + i), way, last_r.at[way, i]).start()
                side_copy(whole).start()
    for i in range(PIECES // 2):
        for way in range(2):
            ref = place(steps, way, way * PIECES // 2 + i)
            take(ref, last_r.at[way, i])
            side_copy(ref).start()
    take(out_g, side_r)
    take(out_g, side_s)
    sent = out_g.at[pl.ds(0, rows * (CHIPS - 1) - rows * half // width)]
    for way in range(2):
        take(sent, ring_s.at[way])
    take(raw_in.at[:, pl.ds(0, RAW)], raw_s)
    take(out_g.at[pl.ds(0, 2 * (rows - RAW)), pl.ds(0, half)], rest_s)
    take(scale_g.at[:, pl.ds(0, half * GROUPS)], scale_s)
    take(slots.at[pl.ds(0, 2 * CHIPS - 1)], slot_s)
    take(pair_slots.at[:, pl.ds(0, CHIPS - 1)], slot_s)
    take(pair_in, pair_s)


def write_kernel(g, u, a, b, g_out, u_out, a_out, b_out, sem):
    parts = 16
    rows = g.shape[0] // parts
    copies = []
    for k in range(parts):
        where = pl.ds(k * rows, rows)
        copies.append(pltpu.make_async_copy(g.at[where], g_out.at[where], sem))
        copies.append(pltpu.make_async_copy(u.at[where], u_out.at[where], sem))
    copies.append(pltpu.make_async_copy(a, a_out, sem))
    copies.append(pltpu.make_async_copy(b, b_out, sem))
    for copy in copies:
        copy.start()
    for copy in copies:
        copy.wait()


def shards(weight_gate, moment_gate, square_gate, weight_up, moment_up, square_up, norm_gain):
    rows, width = weight_gate.shape
    total_rows = rows * lax.axis_size("rows")
    any_spec = pl.BlockSpec(memory_space=pl.ANY)
    hbm_spec = pl.BlockSpec(memory_space=pltpu.HBM)
    vmem_spec = pl.BlockSpec(memory_space=pltpu.VMEM)
    dma = pltpu.SemaphoreType.DMA
    g, u, a, b = pl.pallas_call(
        gather_kernel,
        name="gather",
        out_shape=(
            pltpu.VMEM((total_rows, width), BF16),
            pltpu.VMEM((total_rows, width), BF16),
            pltpu.VMEM((1, width), F32),
            pltpu.VMEM((1, width), F32),
        ),
        in_specs=[hbm_spec] * 7,
        out_specs=(vmem_spec,) * 4,
        scratch_shapes=[
            pltpu.VMEM((2, 3, rows, width), F32),
            pltpu.VMEM((2, rows, width), F32),
            pltpu.VMEM((1, rows), F32),
            pltpu.VMEM((rows, rows), F32),
            pltpu.VMEM((2, 1, width), F32),
            pltpu.VMEM((2 * CHIPS, 1, width // GROUPS), F32),
            pltpu.VMEM((GROUPS - 1, 1, width // GROUPS), F32),
            pltpu.VMEM((GROUPS - 1, CHIPS, 1, width // GROUPS), F32),
            pltpu.VMEM((2, RAW, width // GROUPS), F32),
            dma((AHEAD + 1,)), dma,
            dma, dma((GROUPS - 1,)), dma, dma((GROUPS,)), dma, dma((GROUPS,)),
            dma, dma((2,)), dma, dma((2,)),
            dma((2,)), dma((2, CHIPS // 2 - 1, 2)), dma((2, PIECES // 2)), dma, dma,
        ],
        compiler_params=pltpu.CompilerParams(
            collective_id=0, has_side_effects=True, vmem_limit_bytes=47 * 2**20
        ),
    )(weight_gate, moment_gate, square_gate, weight_up, moment_up, square_up, norm_gain.reshape(1, rows))
    g, u, a, b = pl.pallas_call(
        write_kernel,
        name="write",
        out_shape=(
            jax.ShapeDtypeStruct((total_rows, width), BF16),
            jax.ShapeDtypeStruct((total_rows, width), BF16),
            jax.ShapeDtypeStruct((1, width), F32),
            jax.ShapeDtypeStruct((1, width), F32),
        ),
        in_specs=[vmem_spec] * 4,
        out_specs=(any_spec,) * 4,
        scratch_shapes=[dma],
        compiler_params=pltpu.CompilerParams(vmem_limit_bytes=2 * 2**20),
    )(g, u, a, b)
    return g, u, a.reshape(width), b.reshape(width)


def solution(mesh):
    return jax.shard_map(
        shards,
        mesh=mesh,
        in_specs=(
            P(("trial", "rows"), "cols"),
            P(("trial", "rows"), "cols"),
            P(("trial", "rows"), "cols"),
            P(("trial", "rows"), "cols"),
            P(("trial", "rows"), "cols"),
            P(("trial", "rows"), "cols"),
            P(("trial", "rows")),
        ),
        out_specs=(
            P("trial", "cols"),
            P("trial", "cols"),
            P(("trial", "cols")),
            P(("trial", "cols")),
        ),
        check_vma=False,
    )
```

time: 146 us -> 102 us (0.70)
  Pallas kernels: 0 us -> 101 us
  waiting for transfers between devices: 92.7 us -> 0 us
  blocking collectives: 21.4 us -> 0 us
  between operations: 14.1 us -> 0.64 us
  local copies, waits for them, and re-layouts: 12.2 us -> 0 us
  other arithmetic: 5.47 us -> 0 us
    pallas_call x0 -> x2, Pallas kernels: none -> 101 us  [the longest x1 95.5 us: shards(): pl.pallas_call(gather_kernel, name='gather', out_shape=(pltpu.VMEM((total...]
    all_gather x1 -> x0, waiting for transfers between devices: 92.7 us -> none  [sent_together(): whole, at, done = (lax.all_gather(both, axis, axis=dim, tiled=True), 0, [])]
    all_to_all x1 -> x0, blocking collectives: 21.4 us -> none  [sent_to_all(): return lax.all_to_all(copies, axis, split_axis=0, concat_axis=0, tiled=True)]
    slice x1 -> x0, local copies, waits for them, and re-layouts: 11.9 us -> none  [sent_together(): done.append(lax.slice_in_dim(whole, at, at + a.shape[along], axis=along))]
    reduce_sum x2 -> x0, other arithmetic: 4.21 us -> none  [the longest x1 4.03 us: shards(): jnp.sum(jnp.abs(whole_gained_gate), axis=0)]
  transfers between devices with their start and end apart: 1 -> 0, of which waited for: 1 -> 0; matrix products, arithmetic and copies ran while one was open for 0% -> 0% of each run, Pallas kernels for 0% -> 0%
where the time goes in v2:
time: 102 us
  Pallas kernels  101 us (99%)
    pallas_call x1, Pallas kernels, shards(): pl.pallas_call(gather_kernel, name='gather', out_shape=(pltpu.VMEM((total...  95.5 us
    pallas_call x1, Pallas kernels, shards(): pl.pallas_call(write_kernel, name='write', out_shape=(jax.ShapeDtypeStruc...  5.8 us

profile of v2, /device:TPU:1, one launch (start us, length us, event | category | flops | bytes accessed | tf_op | source)
XLA Modules:
  0.0 101.9 jit_solution(772169909732614145)
XLA Ops:
  0.6 95.5 %gather.1 = (bf16[2048,2048]{1,0:T(8,128)(2,1)S(1)}, bf16[2048,2048]{1,0:T(8,128)(2,1)S(1)}, f32[1,2048]{1,0:T(1,128)S(1)}, f32[1,2048]{1,0:T(1,128)S(1)}) custom-call(f32[128,2048]{1,0:T(8,128)} %wg.1, f32[128,2048]{1,0:T(8,128)} %mg.1, f32[128,2048]{1,0:T(8,128)} %sg.1, f32[128,2048]{1,0:T(8,128)} %wu.1, f32[128,2048]{1,0:T(8,128)} %mu.1, f32[128,2048]{1,0:T(8,128)} %su.1, ...), custom_call_target="tpu_custom_call" | custom-call | tf_op jit(solution)/shard_map/gather/pallas_call | solution.py:301
  96.1 5.8 %write.1 = (bf16[2048,2048]{1,0:T(8,128)(2,1)}, bf16[2048,2048]{1,0:T(8,128)(2,1)}, f32[1,2048]{1,0:T(1,128)}, f32[1,2048]{1,0:T(1,128)}) custom-call(bf16[2048,2048]{1,0:T(8,128)(2,1)S(1)} %get-tuple-element.12.g, bf16[2048,2048]{1,0:T(8,128)(2,1)S(1)} %get-tuple-element.13.u, f32[1,2048]{1,0:T(1,128)S(1)} %get-tuple-element.14.a, ...), custom_call_target="tpu_custom_call" | custom-call | tf_op jit(solution)/shard_map/write/pallas_call | solution.py:331

commit v3 on v2

--- a/solution.py
+++ b/solution.py
@@ -20,8 +20,9 @@
 PIECES = 8
 CHUNK = 512
 AHEAD = 3
-RAW = 48
-SLICE = 16
+RAW = 64
+SLICES = ((0,), (1,), (), ())
+SLICE = 32
 
 
 def gather_kernel(
@@ -114,47 +115,60 @@
         first_copy(cols_of(0, 1), partner).start()
         slots[me] = part[0, :, cols_of(0, 0)]
 
+    rest = range(1, GROUPS)
+
     def pair_copy(g):
         return pltpu.make_async_remote_copy(
             src_ref=part_of(g, cols_of(g, 1)), dst_ref=pair_in.at[g - 1],
-            send_sem=pair_s, recv_sem=pair_r.at[g - 1], **device(partner),
-        )
-
-    def send_pair(g):
-        pair_copy(g).wait_recv()
-        pair_slots[g - 1, chip] = part[g // (GROUPS // 2), :, cols_of(g, 0)] + pair_in[g - 1]
-        ref = pair_slots.at[g - 1, chip]
+            send_sem=pair_s, recv_sem=pair_r, **device(partner),
+        )
+
+    def send_rest():
+        take(pair_in, pair_r)
+        for g in rest:
+            pair_slots[chip, g - 1] = part_of(g, cols_of(g, 0))[...] + pair_in[g - 1]
+        ref = pair_slots.at[chip]
         for d in far_first:
             pltpu.make_async_remote_copy(
-                src_ref=ref, dst_ref=ref, send_sem=slot_s, recv_sem=slot_r.at[g],
+                src_ref=ref, dst_ref=ref, send_sem=slot_s, recv_sem=slot_r.at[1],
                 **device(at(chip + d) * 2 + core),
             ).start()
 
-    def scale_copy(g, h):
-        ref = scales[g // (GROUPS // 2)].at[:, cols_of(g, h)]
-        return pltpu.make_async_remote_copy(
-            src_ref=ref, dst_ref=ref, send_sem=scale_s, recv_sem=scale_r.at[g],
+    def scale_copy(g):
+        ref = scales[g // (GROUPS // 2)].at[:, cols_of(g, 0)]
+        return pltpu.make_async_remote_copy(
+            src_ref=ref, dst_ref=ref, send_sem=scale_s, recv_sem=scale_r.at[min(g, 1)],
             **device(partner),
         )
 
-    def total(g):
-        mine = slots if g == 0 else pair_slots.at[g - 1]
-        count = mine.shape[0]
-        take(mine.at[pl.ds(0, count - 1)], slot_r.at[g])
-        acc = mine[0]
-        for r in range(1, count):
-            acc = acc + mine[r]
-        scales[g // (GROUPS // 2)][:, cols_of(g, 0)] = acc / D_MODEL
-        scale_copy(g, 0).start()
+    def total_first():
+        take(slots.at[pl.ds(0, 2 * CHIPS - 1)], slot_r.at[0])
+        acc = slots[0]
+        for r in range(1, 2 * CHIPS):
+            acc = acc + slots[r]
+        scale_g[:, cols_of(0, 0)] = acc / D_MODEL
+        scale_copy(0).start()
+
+    def total_rest():
+        take(pair_slots.at[pl.ds(0, CHIPS - 1)], slot_r.at[1])
+        for g in rest:
+            acc = pair_slots[0, g - 1]
+            for r in range(1, CHIPS):
+                acc = acc + pair_slots[r, g - 1]
+            scales[g // (GROUPS // 2)][:, cols_of(g, 0)] = acc / D_MODEL
+            scale_copy(g).start()
 
     def rows_of(offset, first=0, count=rows):
         start = (at(chip + offset) * 2 + core) * rows + first
         return pl.ds(pl.multiple_of(start, SLICE), count)
 
-    def place(offset, q, p=None, first=0, count=rows):
-        if p is None:
-            return outs[q].at[rows_of(offset, first, count)]
-        return outs[q].at[rows_of(offset, first, count), cols_of(p // 2, p % 2)]
+    def place(offset, g):
+        cols = pl.ds((g % (GROUPS // 2)) * wide, wide)
+        return outs[g * 2 // GROUPS].at[rows_of(offset), cols]
+
+    def quarter(offset, g, i):
+        cols = pl.ds((g % (GROUPS // 2)) * wide + i * half, half)
+        return outs[g * 2 // GROUPS].at[rows_of(offset), cols]
 
     def neighbour(way):
         return device(at(chip + 1 - 2 * way) * 2 + core)
@@ -172,8 +186,8 @@
             send_sem=raw_s, recv_sem=raw_r.at[way], **neighbour(way),
         )
 
-    def send_raw(i):
-        if i < RAW // SLICE:
+    def send_raw(turn):
+        for i in SLICES[turn]:
             for way in range(2):
                 raw_copy(i, way).start()
 
@@ -194,42 +208,51 @@
             inverse = 1.0 / scales[q][:, cols]
             outs[q][pl.ds(start, rows), cols] = (plain[q, :, cols] * inverse).astype(BF16)
 
+    def send_way(p, way):
+        g = p // 2
+        if p == 0:
+            ref = outs[0].at[rows_of(0, RAW, rows - RAW), cols_of(0, 0)]
+            onward(ref, way, rest_r.at[way], rest_s).start()
+        else:
+            ref = outs[g * 2 // GROUPS].at[rows_of(0), cols_of(g, p % 2)]
+            onward(ref, way, ring_r.at[way, 0, g]).start()
+
     def send_own(p):
+        g = p // 2
         narrow(p)
-        q = p * 2 // PIECES
-        for way in range(2):
-            if p == 0:
-                onward(place(0, q, p, RAW, rows - RAW), way, rest_r.at[way], rest_s).start()
-            else:
-                onward(place(0, q, p), way, ring_r.at[way, 0, q]).start()
-        side_copy(place(0, q, p)).start()
-
+        send_way(p, 0)
+        if g != late:
+            send_way(p, 1)
+        side_copy(outs[g * 2 // GROUPS].at[rows_of(0), cols_of(g, p % 2)]).start()
+
+    late = 1
+    orders = ((0, 1, 2, 3), (0, 2, 3, 1))
     each = 2 * chunks // GROUPS
     for n in range(each):
         update(n)
     pl.semaphore_wait(barrier, 2 * CHIPS - 1)
     send_first()
     send_raw(0)
-    for g in range(1, GROUPS):
+    for g in rest:
         for n in range(g * each, (g + 1) * each):
             update(n)
         pair_copy(g).start()
-        if g > 1:
-            send_pair(g - 1)
-            send_raw(g - 1)
-    send_pair(GROUPS - 1)
-    total(0)
+        send_raw(g)
+    send_rest()
+    total_first()
     send_own(0)
-    scale_copy(0, 1).wait_recv()
+    take(scale_g.at[:, cols_of(0, 0)], scale_r.at[0])
     send_own(1)
-    for g in range(1, GROUPS):
-        total(g)
-        send_own(2 * g)
-        scale_copy(g, 1).wait_recv()
-        send_own(2 * g + 1)
+    total_rest()
+    send_own(2)
+    take(scale_g.at[:, pl.ds(0, half * (GROUPS - 1))], scale_r.at[1])
+    for p in range(3, PIECES):
+        send_own(p)
+    for h in range(2):
+        send_way(2 * late + h, 1)
     def scale_raw(way):
         take(raw_in.at[way, pl.ds(0, RAW)], raw_r.at[way])
-        take(place(0, 0, 0, RAW, rows - RAW), rest_r.at[way])
+        take(out_g.at[pl.ds(0, rows - RAW), pl.ds(0, half)], rest_r.at[way])
 
         @pl.loop(0, half // 128)
         def _(j):
@@ -241,26 +264,29 @@
             ).astype(BF16)
 
     steps = CHIPS // 2
+    farthest = ((0, 1), (2, 3))
     for step in range(steps - 1):
-        for q in range(2):
+        for turn in range(GROUPS):
             for way in range(2):
+                g = orders[way][turn]
                 offset = (2 * way - 1) * (step + 1)
-                whole = place(offset, q)
-                if step == 0 and q == 0:
+                whole = place(offset, g)
+                if step == 0 and g == 0:
                     scale_raw(way)
-                    take(outs[q].at[rows_of(offset), pl.ds(0, width - half)], ring_r.at[way, step, q])
+                    take(quarter(offset, g, 0), ring_r.at[way, step, g])
                 else:
-                    take(whole, ring_r.at[way, step, q])
+                    take(whole, ring_r.at[way, step, g])
                 if step + 1 < steps - 1:
-                    onward(whole, way, ring_r.at[way, step + 1, q]).start()
-                elif q == way:
-                    for i in range(PIECES // 2):
-                        onward(place(offset, q, q * PIECES // 2 + i), way, last_r.at[way, i]).start()
+                    onward(whole, way, ring_r.at[way, step + 1, g]).start()
+                elif g in farthest[way]:
+                    for i in range(2):
+                        k = farthest[way].index(g) * 2 + i
+                        onward(quarter(offset, g, i), way, last_r.at[way, k]).start()
                 side_copy(whole).start()
-    for i in range(PIECES // 2):
+    for k in range(PIECES // 2):
         for way in range(2):
-            ref = place(steps, way, way * PIECES // 2 + i)
-            take(ref, last_r.at[way, i])
+            ref = quarter(steps, farthest[way][k // 2], k % 2)
+            take(ref, last_r.at[way, k])
             side_copy(ref).start()
     take(out_g, side_r)
     take(out_g, side_s)
@@ -271,7 +297,7 @@
     take(out_g.at[pl.ds(0, 2 * (rows - RAW)), pl.ds(0, half)], rest_s)
     take(scale_g.at[:, pl.ds(0, half * GROUPS)], scale_s)
     take(slots.at[pl.ds(0, 2 * CHIPS - 1)], slot_s)
-    take(pair_slots.at[:, pl.ds(0, CHIPS - 1)], slot_s)
+    take(pair_slots.at[pl.ds(0, CHIPS - 1)], slot_s)
     take(pair_in, pair_s)
 
 
@@ -317,12 +343,12 @@
             pltpu.VMEM((2, 1, width), F32),
             pltpu.VMEM((2 * CHIPS, 1, width // GROUPS), F32),
             pltpu.VMEM((GROUPS - 1, 1, width // GROUPS), F32),
-            pltpu.VMEM((GROUPS - 1, CHIPS, 1, width // GROUPS), F32),
+            pltpu.VMEM((CHIPS, GROUPS - 1, 1, width // GROUPS), F32),
             pltpu.VMEM((2, RAW, width // GROUPS), F32),
             dma((AHEAD + 1,)), dma,
-            dma, dma((GROUPS - 1,)), dma, dma((GROUPS,)), dma, dma((GROUPS,)),
+            dma, dma, dma, dma((2,)), dma, dma((2,)),
             dma, dma((2,)), dma, dma((2,)),
-            dma((2,)), dma((2, CHIPS // 2 - 1, 2)), dma((2, PIECES // 2)), dma, dma,
+            dma((2,)), dma((2, CHIPS // 2 - 1, GROUPS)), dma((2, PIECES // 2)), dma, dma,
         ],
         compiler_params=pltpu.CompilerParams(
             collective_id=0, has_side_effects=True, vmem_limit_bytes=47 * 2**20

time: 102 us -> 101 us (level)
  no operation moved by 1% of the time
where the time goes in v3:
time: 101 us
  Pallas kernels  101 us (100%)
    pallas_call x1, Pallas kernels, shards(): pl.pallas_call(gather_kernel, name='gather', out_shape=(pltpu.VMEM((total...  94.9 us
    pallas_call x1, Pallas kernels, shards(): pl.pallas_call(write_kernel, name='write', out_shape=(jax.ShapeDtypeStruc...  5.8 us

profile of v3, /device:TPU:1, one launch (start us, length us, event | category | flops | bytes accessed | tf_op | source)
XLA Modules:
  0.0 101.3 jit_solution(8794501085576469215)
XLA Ops:
  0.6 94.9 %gather.1 = (bf16[2048,2048]{1,0:T(8,128)(2,1)S(1)}, bf16[2048,2048]{1,0:T(8,128)(2,1)S(1)}, f32[1,2048]{1,0:T(1,128)S(1)}, f32[1,2048]{1,0:T(1,128)S(1)}) custom-call(f32[128,2048]{1,0:T(8,128)} %wg.1, f32[128,2048]{1,0:T(8,128)} %mg.1, f32[128,2048]{1,0:T(8,128)} %sg.1, f32[128,2048]{1,0:T(8,128)} %wu.1, f32[128,2048]{1,0:T(8,128)} %mu.1, f32[128,2048]{1,0:T(8,128)} %su.1, ...), custom_call_target="tpu_custom_call" | custom-call | tf_op jit(solution)/shard_map/gather/pallas_call | solution.py:327
  95.5 5.8 %write.1 = (bf16[2048,2048]{1,0:T(8,128)(2,1)}, bf16[2048,2048]{1,0:T(8,128)(2,1)}, f32[1,2048]{1,0:T(1,128)}, f32[1,2048]{1,0:T(1,128)}) custom-call(bf16[2048,2048]{1,0:T(8,128)(2,1)S(1)} %get-tuple-element.12.g, bf16[2048,2048]{1,0:T(8,128)(2,1)S(1)} %get-tuple-element.13.u, f32[1,2048]{1,0:T(1,128)S(1)} %get-tuple-element.14.a, ...), custom_call_target="tpu_custom_call" | custom-call | tf_op jit(solution)/shard_map/write/pallas_call | solution.py:357

commit v4 on v3

--- a/solution.py
+++ b/solution.py
@@ -29,8 +29,7 @@
     wg, mg, sg, wu, mu, su, gain_hbm,
     out_g, out_u, scale_g, scale_u,
     held, plain, gain, gain_t, part, slots, pair_in, pair_slots, raw_in,
-    load_sem, gain_sem, pair_s, pair_r, slot_s, slot_r, scale_s, scale_r,
-    raw_s, raw_r, rest_s, rest_r, ring_s, ring_r, last_r, side_s, side_r,
+    load_sem, gain_sem, sent, pair_r, slot_r, scale_r, raw_r, rest_r, ring_r, last_r, side_r,
 ):
     rows, width = wg.shape
     wide = width * 2 // GROUPS
@@ -105,7 +104,7 @@
     def first_copy(where, target):
         return pltpu.make_async_remote_copy(
             src_ref=part_of(0, where), dst_ref=slots.at[me],
-            send_sem=slot_s, recv_sem=slot_r.at[0], **device(target),
+            send_sem=sent, recv_sem=slot_r.at[0], **device(target),
         )
 
     def send_first():
@@ -120,7 +119,7 @@
     def pair_copy(g):
         return pltpu.make_async_remote_copy(
             src_ref=part_of(g, cols_of(g, 1)), dst_ref=pair_in.at[g - 1],
-            send_sem=pair_s, recv_sem=pair_r, **device(partner),
+            send_sem=sent, recv_sem=pair_r, **device(partner),
         )
 
     def send_rest():
@@ -130,14 +129,14 @@
         ref = pair_slots.at[chip]
         for d in far_first:
             pltpu.make_async_remote_copy(
-                src_ref=ref, dst_ref=ref, send_sem=slot_s, recv_sem=slot_r.at[1],
+                src_ref=ref, dst_ref=ref, send_sem=sent, recv_sem=slot_r.at[1],
                 **device(at(chip + d) * 2 + core),
             ).start()
 
     def scale_copy(g):
         ref = scales[g // (GROUPS // 2)].at[:, cols_of(g, 0)]
         return pltpu.make_async_remote_copy(
-            src_ref=ref, dst_ref=ref, send_sem=scale_s, recv_sem=scale_r.at[min(g, 1)],
+            src_ref=ref, dst_ref=ref, send_sem=sent, recv_sem=scale_r.at[min(g, 1)],
             **device(partner),
         )
 
@@ -173,17 +172,16 @@
     def neighbour(way):
         return device(at(chip + 1 - 2 * way) * 2 + core)
 
-    def onward(ref, way, recv_sem, send_sem=None):
-        return pltpu.make_async_remote_copy(
-            src_ref=ref, dst_ref=ref, send_sem=ring_s.at[way] if send_sem is None else send_sem,
-            recv_sem=recv_sem, **neighbour(way),
+    def onward(ref, way, recv_sem):
+        return pltpu.make_async_remote_copy(
+            src_ref=ref, dst_ref=ref, send_sem=sent, recv_sem=recv_sem, **neighbour(way)
         )
 
     def raw_copy(i, way):
         some = pl.ds(i * SLICE, SLICE)
         return pltpu.make_async_remote_copy(
             src_ref=plain.at[0, some, cols_of(0, 0)], dst_ref=raw_in.at[way, some],
-            send_sem=raw_s, recv_sem=raw_r.at[way], **neighbour(way),
+            send_sem=sent, recv_sem=raw_r.at[way], **neighbour(way),
         )
 
     def send_raw(turn):
@@ -193,7 +191,7 @@
 
     def side_copy(ref):
         return pltpu.make_async_remote_copy(
-            src_ref=ref, dst_ref=ref, send_sem=side_s, recv_sem=side_r, **device(partner)
+            src_ref=ref, dst_ref=ref, send_sem=sent, recv_sem=side_r, **device(partner)
         )
 
     def narrow(p):
@@ -208,14 +206,17 @@
             inverse = 1.0 / scales[q][:, cols]
             outs[q][pl.ds(start, rows), cols] = (plain[q, :, cols] * inverse).astype(BF16)
 
+    def unit_of(g, way):
+        return orders[way].index(g) // 2
+
     def send_way(p, way):
         g = p // 2
         if p == 0:
             ref = outs[0].at[rows_of(0, RAW, rows - RAW), cols_of(0, 0)]
-            onward(ref, way, rest_r.at[way], rest_s).start()
+            onward(ref, way, rest_r.at[way]).start()
         else:
             ref = outs[g * 2 // GROUPS].at[rows_of(0), cols_of(g, p % 2)]
-            onward(ref, way, ring_r.at[way, 0, g]).start()
+            onward(ref, way, ring_r.at[way, 0, unit_of(g, way)]).start()
 
     def send_own(p):
         g = p // 2
@@ -266,39 +267,38 @@
     steps = CHIPS // 2
     farthest = ((0, 1), (2, 3))
     for step in range(steps - 1):
-        for turn in range(GROUPS):
+        for unit in range(2):
             for way in range(2):
-                g = orders[way][turn]
                 offset = (2 * way - 1) * (step + 1)
-                whole = place(offset, g)
-                if step == 0 and g == 0:
+                groups = orders[way][2 * unit : 2 * unit + 2]
+                if step == 0 and unit == 0:
                     scale_raw(way)
-                    take(quarter(offset, g, 0), ring_r.at[way, step, g])
+                    take(out_g.at[pl.ds(0, rows), pl.ds(0, width - half)], ring_r.at[way, step, unit])
                 else:
-                    take(whole, ring_r.at[way, step, g])
-                if step + 1 < steps - 1:
-                    onward(whole, way, ring_r.at[way, step + 1, g]).start()
-                elif g in farthest[way]:
-                    for i in range(2):
-                        k = farthest[way].index(g) * 2 + i
-                        onward(quarter(offset, g, i), way, last_r.at[way, k]).start()
-                side_copy(whole).start()
+                    take(out_g.at[pl.ds(0, rows)], ring_r.at[way, step, unit])
+                for g in groups:
+                    if step + 1 < steps - 1:
+                        onward(place(offset, g), way, ring_r.at[way, step + 1, unit]).start()
+                    elif g in farthest[way]:
+                        for i in range(2):
+                            k = farthest[way].index(g) * 2 + i
+                            onward(quarter(offset, g, i), way, last_r.at[way, k]).start()
+                    side_copy(place(offset, g)).start()
     for k in range(PIECES // 2):
         for way in range(2):
             ref = quarter(steps, farthest[way][k // 2], k % 2)
             take(ref, last_r.at[way, k])
             side_copy(ref).start()
     take(out_g, side_r)
-    take(out_g, side_s)
-    sent = out_g.at[pl.ds(0, rows * (CHIPS - 1) - rows * half // width)]
+    take(out_g, sent)
     for way in range(2):
-        take(sent, ring_s.at[way])
-    take(raw_in.at[:, pl.ds(0, RAW)], raw_s)
-    take(out_g.at[pl.ds(0, 2 * (rows - RAW)), pl.ds(0, half)], rest_s)
-    take(scale_g.at[:, pl.ds(0, half * GROUPS)], scale_s)
-    take(slots.at[pl.ds(0, 2 * CHIPS - 1)], slot_s)
-    take(pair_slots.at[pl.ds(0, CHIPS - 1)], slot_s)
-    take(pair_in, pair_s)
+        take(out_g.at[pl.ds(0, rows * (CHIPS - 1) - rows * half // width)], sent)
+    take(raw_in, sent)
+    take(out_g.at[pl.ds(0, 2 * (rows - RAW)), pl.ds(0, half)], sent)
+    take(scale_g.at[:, pl.ds(0, half * GROUPS)], sent)
+    take(slots.at[pl.ds(0, 2 * CHIPS - 1)], sent)
+    take(pair_slots.at[pl.ds(0, CHIPS - 1)], sent)
+    take(pair_in, sent)
 
 
 def write_kernel(g, u, a, b, g_out, u_out, a_out, b_out, sem):
@@ -345,10 +345,8 @@
             pltpu.VMEM((GROUPS - 1, 1, width // GROUPS), F32),
             pltpu.VMEM((CHIPS, GROUPS - 1, 1, width // GROUPS), F32),
             pltpu.VMEM((2, RAW, width // GROUPS), F32),
-            dma((AHEAD + 1,)), dma,
-            dma, dma, dma, dma((2,)), dma, dma((2,)),
-            dma, dma((2,)), dma, dma((2,)),
-            dma((2,)), dma((2, CHIPS // 2 - 1, GROUPS)), dma((2, PIECES // 2)), dma, dma,
+            dma((AHEAD + 1,)), dma, dma, dma, dma((2,)), dma((2,)), dma((2,)), dma((2,)),
+            dma((2, CHIPS // 2 - 1, 2)), dma((2, PIECES // 2)), dma,
         ],
         compiler_params=pltpu.CompilerParams(
             collective_id=0, has_side_effects=True, vmem_limit_bytes=47 * 2**20

time: 101 us -> 101 us (level)
  no operation moved by 1% of the time
where the time goes in v4:
time: 101 us
  Pallas kernels  100 us (99%)
    pallas_call x1, Pallas kernels, shards(): pl.pallas_call(gather_kernel, name='gather', out_shape=(pltpu.VMEM((total...  94.7 us
    pallas_call x1, Pallas kernels, shards(): pl.pallas_call(write_kernel, name='write', out_shape=(jax.ShapeDtypeStruc...  5.8 us

profile of v4, /device:TPU:1, one launch (start us, length us, event | category | flops | bytes accessed | tf_op | source)
XLA Modules:
  0.0 101.1 jit_solution(153645704326708326)
XLA Ops:
  0.6 94.7 %gather.1 = (bf16[2048,2048]{1,0:T(8,128)(2,1)S(1)}, bf16[2048,2048]{1,0:T(8,128)(2,1)S(1)}, f32[1,2048]{1,0:T(1,128)S(1)}, f32[1,2048]{1,0:T(1,128)S(1)}) custom-call(f32[128,2048]{1,0:T(8,128)} %wg.1, f32[128,2048]{1,0:T(8,128)} %mg.1, f32[128,2048]{1,0:T(8,128)} %sg.1, f32[128,2048]{1,0:T(8,128)} %wu.1, f32[128,2048]{1,0:T(8,128)} %mu.1, f32[128,2048]{1,0:T(8,128)} %su.1, ...), custom_call_target="tpu_custom_call" | custom-call | tf_op jit(solution)/shard_map/gather/pallas_call | solution.py:327
  95.3 5.8 %write.1 = (bf16[2048,2048]{1,0:T(8,128)(2,1)}, bf16[2048,2048]{1,0:T(8,128)(2,1)}, f32[1,2048]{1,0:T(1,128)}, f32[1,2048]{1,0:T(1,128)}) custom-call(bf16[2048,2048]{1,0:T(8,128)(2,1)S(1)} %get-tuple-element.12.g, bf16[2048,2048]{1,0:T(8,128)(2,1)S(1)} %get-tuple-element.13.u, f32[1,2048]{1,0:T(1,128)S(1)} %get-tuple-element.14.a, ...), custom_call_target="tpu_custom_call" | custom-call | tf_op jit(solution)/shard_map/write/pallas_call | solution.py:355

commit v5 on v4

--- a/solution.py
+++ b/solution.py
@@ -20,9 +20,9 @@
 PIECES = 8
 CHUNK = 512
 AHEAD = 3
-RAW = 64
-SLICES = ((0,), (1,), (), ())
-SLICE = 32
+RAW = 80
+SLICES = ((0, 1, 2), (), (), (3, 4))
+SLICE = 16
 
 
 def gather_kernel(
@@ -58,16 +58,16 @@
                 sources[q][i].at[:, cols], held.at[q, i, :, cols], load_sem.at[n % (AHEAD + 1)]
             ).start()
 
-    gain_copy = pltpu.make_async_copy(gain_hbm, gain, gain_sem)
-    gain_copy.start()
-    for n in range(AHEAD):
-        load(n)
-
     barrier = pltpu.get_barrier_semaphore()
     for d in (4, 3, 5, 2, 6, 1, 7):
         for h in range(2):
             pl.semaphore_signal(barrier, inc=1, **device(at(chip + d) * 2 + h))
     pl.semaphore_signal(barrier, inc=1, **device(partner))
+
+    gain_copy = pltpu.make_async_copy(gain_hbm, gain, gain_sem)
+    gain_copy.start()
+    for n in range(AHEAD):
+        load(n)
 
     gain_copy.wait()
     gain_t[...] = jnp.broadcast_to(gain[...], (rows, rows)).T
@@ -238,8 +238,10 @@
         for n in range(g * each, (g + 1) * each):
             update(n)
         pair_copy(g).start()
-        send_raw(g)
+        if g < GROUPS - 1:
+            send_raw(g)
     send_rest()
+    send_raw(GROUPS - 1)
     total_first()
     send_own(0)
     take(scale_g.at[:, cols_of(0, 0)], scale_r.at[0])

time: 101 us -> 101 us (level)
  no operation moved by 1% of the time
where the time goes in v5:
time: 101 us
  Pallas kernels  100 us (99%)
    pallas_call x1, Pallas kernels, shards(): pl.pallas_call(gather_kernel, name='gather', out_shape=(pltpu.VMEM((total...  94.6 us
    pallas_call x1, Pallas kernels, shards(): pl.pallas_call(write_kernel, name='write', out_shape=(jax.ShapeDtypeStruc...  5.8 us

profile of v5, /device:TPU:1, one launch (start us, length us, event | category | flops | bytes accessed | tf_op | source)
XLA Modules:
  0.0 101.0 jit_solution(15410396389692601540)
XLA Ops:
  0.6 94.6 %gather.1 = (bf16[2048,2048]{1,0:T(8,128)(2,1)S(1)}, bf16[2048,2048]{1,0:T(8,128)(2,1)S(1)}, f32[1,2048]{1,0:T(1,128)S(1)}, f32[1,2048]{1,0:T(1,128)S(1)}) custom-call(f32[128,2048]{1,0:T(8,128)} %wg.1, f32[128,2048]{1,0:T(8,128)} %mg.1, f32[128,2048]{1,0:T(8,128)} %sg.1, f32[128,2048]{1,0:T(8,128)} %wu.1, f32[128,2048]{1,0:T(8,128)} %mu.1, f32[128,2048]{1,0:T(8,128)} %su.1, ...), custom_call_target="tpu_custom_call" | custom-call | tf_op jit(solution)/shard_map/gather/pallas_call | solution.py:329
  95.2 5.8 %write.1 = (bf16[2048,2048]{1,0:T(8,128)(2,1)}, bf16[2048,2048]{1,0:T(8,128)(2,1)}, f32[1,2048]{1,0:T(1,128)}, f32[1,2048]{1,0:T(1,128)}) custom-call(bf16[2048,2048]{1,0:T(8,128)(2,1)S(1)} %get-tuple-element.12.g, bf16[2048,2048]{1,0:T(8,128)(2,1)S(1)} %get-tuple-element.13.u, f32[1,2048]{1,0:T(1,128)S(1)} %get-tuple-element.14.a, ...), custom_call_target="tpu_custom_call" | custom-call | tf_op jit(solution)/shard_map/write/pallas_call | solution.py:357

commit v6 on v5

--- a/solution.py
+++ b/solution.py
@@ -18,6 +18,7 @@
 CHIPS = 8
 GROUPS = 4
 PIECES = 8
+LAST = 5
 CHUNK = 512
 AHEAD = 3
 RAW = 80
@@ -163,10 +164,6 @@
 
     def place(offset, g):
         cols = pl.ds((g % (GROUPS // 2)) * wide, wide)
-        return outs[g * 2 // GROUPS].at[rows_of(offset), cols]
-
-    def quarter(offset, g, i):
-        cols = pl.ds((g % (GROUPS // 2)) * wide + i * half, half)
         return outs[g * 2 // GROUPS].at[rows_of(offset), cols]
 
     def neighbour(way):
@@ -268,6 +265,17 @@
 
     steps = CHIPS // 2
     farthest = ((0, 1), (2, 3))
+
+    def last_pieces(offset, way, g):
+        if g == farthest[way][0]:
+            return [(0, place(offset, g))]
+        cols = [pl.ds((g % (GROUPS // 2)) * wide + i * half, half) for i in range(2)]
+        return [
+            (1 + 2 * i + j, outs[g * 2 // GROUPS].at[rows_of(offset, j * rows // 2, rows // 2), cols[i]])
+            for i in range(2)
+            for j in range(2)
+        ]
+
     for step in range(steps - 1):
         for unit in range(2):
             for way in range(2):
@@ -282,13 +290,12 @@
                     if step + 1 < steps - 1:
                         onward(place(offset, g), way, ring_r.at[way, step + 1, unit]).start()
                     elif g in farthest[way]:
-                        for i in range(2):
-                            k = farthest[way].index(g) * 2 + i
-                            onward(quarter(offset, g, i), way, last_r.at[way, k]).start()
+                        for k, ref in last_pieces(offset, way, g):
+                            onward(ref, way, last_r.at[way, k]).start()
                     side_copy(place(offset, g)).start()
-    for k in range(PIECES // 2):
+    for turn in range(LAST):
         for way in range(2):
-            ref = quarter(steps, farthest[way][k // 2], k % 2)
+            k, ref = [piece for g in farthest[way] for piece in last_pieces(steps, way, g)][turn]
             take(ref, last_r.at[way, k])
             side_copy(ref).start()
     take(out_g, side_r)
@@ -304,7 +311,7 @@
 
 
 def write_kernel(g, u, a, b, g_out, u_out, a_out, b_out, sem):
-    parts = 16
+    parts = 32
     rows = g.shape[0] // parts
     copies = []
     for k in range(parts):
@@ -348,7 +355,7 @@
             pltpu.VMEM((CHIPS, GROUPS - 1, 1, width // GROUPS), F32),
             pltpu.VMEM((2, RAW, width // GROUPS), F32),
             dma((AHEAD + 1,)), dma, dma, dma, dma((2,)), dma((2,)), dma((2,)), dma((2,)),
-            dma((2, CHIPS // 2 - 1, 2)), dma((2, PIECES // 2)), dma,
+            dma((2, CHIPS // 2 - 1, 2)), dma((2, LAST)), dma,
         ],
         compiler_params=pltpu.CompilerParams(
             collective_id=0, has_side_effects=True, vmem_limit_bytes=47 * 2**20

time: 101 us -> 101 us (level)
  no operation moved by 1% of the time
where the time goes in v6:
time: 101 us
  Pallas kernels  100 us (99%)
    pallas_call x1, Pallas kernels, shards(): pl.pallas_call(gather_kernel, name='gather', out_shape=(pltpu.VMEM((total...  94.4 us
    pallas_call x1, Pallas kernels, shards(): pl.pallas_call(write_kernel, name='write', out_shape=(jax.ShapeDtypeStruc...  5.77 us

profile of v6, /device:TPU:1, one launch (start us, length us, event | category | flops | bytes accessed | tf_op | source)
XLA Modules:
  0.0 100.8 jit_solution(16838681190659099910)
XLA Ops:
  0.6 94.4 %gather.1 = (bf16[2048,2048]{1,0:T(8,128)(2,1)S(1)}, bf16[2048,2048]{1,0:T(8,128)(2,1)S(1)}, f32[1,2048]{1,0:T(1,128)S(1)}, f32[1,2048]{1,0:T(1,128)S(1)}) custom-call(f32[128,2048]{1,0:T(8,128)} %wg.1, f32[128,2048]{1,0:T(8,128)} %mg.1, f32[128,2048]{1,0:T(8,128)} %sg.1, f32[128,2048]{1,0:T(8,128)} %wu.1, f32[128,2048]{1,0:T(8,128)} %mu.1, f32[128,2048]{1,0:T(8,128)} %su.1, ...), custom_call_target="tpu_custom_call" | custom-call | tf_op jit(solution)/shard_map/gather/pallas_call | solution.py:336
  95.0 5.8 %write.1 = (bf16[2048,2048]{1,0:T(8,128)(2,1)}, bf16[2048,2048]{1,0:T(8,128)(2,1)}, f32[1,2048]{1,0:T(1,128)}, f32[1,2048]{1,0:T(1,128)}) custom-call(bf16[2048,2048]{1,0:T(8,128)(2,1)S(1)} %get-tuple-element.12.g, bf16[2048,2048]{1,0:T(8,128)(2,1)S(1)} %get-tuple-element.13.u, f32[1,2048]{1,0:T(1,128)S(1)} %get-tuple-element.14.a, ...), custom_call_target="tpu_custom_call" | custom-call | tf_op jit(solution)/shard_map/write/pallas_call | solution.py:364
